TPU v7x, 64 devices: a 2x2x8 block of a 4x4x8 slice. The times are simulated.
64 devices in a mesh: dp: 4 (over x, y), ep: 16 (over z, core).
Axes of the slice: x: 2, y: 2, z: 8, core: 2. Of those that a mesh axis runs over, the one named last changes fastest.
The devices are a block of a 4x4x8 slice.
Arguments:
- hidden_in: bfloat16 [32768, 2048], P(('dp', 'ep')), parts along dimension 0
- topk_idx: int32 [32768, 6], P(('dp', 'ep')), parts along dimension 0
- norm_gain: bfloat16 [2048], replicated
- w_router: bfloat16 [2048, 64], replicated
- w_sgate: bfloat16 [2048, 1], replicated
- s_gate: bfloat16 [2048, 2816], replicated
- s_up: bfloat16 [2048, 2816], replicated
- s_down: bfloat16 [2816, 2048], replicated
- w_gate: bfloat16 [64, 2048, 1408], P('ep')
- w_up: bfloat16 [64, 2048, 1408], P('ep')
- w_down: bfloat16 [64, 1408, 2048], P('ep')
Outputs:
- output: bfloat16 [32768, 2048], P(('dp', 'ep')), parts along dimension 0
There are 4 independent parts. A program takes and returns all parts, laid end to end along the dimension named above; an argument that names none is the same for every part.
All inputs are finite; a program needn't handle non-finite values.
Results may differ from a plain program's by a relative error of at most 0.00125.
Values are sent between devices in bfloat16 or wider.
A program may use at most 768 MiB of HBM per device.

v0:
```python
import jax
import jax.numpy as jnp
from jax import lax
from jax.sharding import PartitionSpec as P


def rms_norm(hidden_in, norm_gain):
    x_f32 = hidden_in.astype(jnp.float32)
    inv_rms = lax.rsqrt(jnp.mean(x_f32 * x_f32, axis=-1, keepdims=True) + 1e-6)
    return (x_f32 * inv_rms * norm_gain.astype(jnp.float32)).astype(jnp.bfloat16)


def shared_expert(normed, w_sgate, s_gate, s_up, s_down):
    shared_act = (jax.nn.silu(jnp.dot(normed, s_gate, preferred_element_type=jnp.float32))
                  * jnp.dot(normed, s_up, preferred_element_type=jnp.float32)).astype(jnp.bfloat16)
    shared_val = jnp.dot(shared_act, s_down, preferred_element_type=jnp.float32)
    return jax.nn.sigmoid(jnp.dot(normed, w_sgate, preferred_element_type=jnp.float32)) * shared_val


def solution(mesh):
    group_size = mesh.shape['ep']

    def device_block(hidden_in, topk_idx, norm_gain, w_router, w_sgate, s_gate, s_up, s_down, w_gate, w_up, w_down):
        tok_dev, hidden = hidden_in.shape
        top_k = topk_idx.shape[1]
        experts = w_router.shape[1]
        slots_dev = w_gate.shape[0]
        num_slots = slots_dev * group_size
        capacity = (5 * tok_dev * group_size * top_k + 4 * experts - 1) // (4 * experts)
        local_max = (2 * tok_dev * top_k + experts - 1) // experts
        normed = rms_norm(hidden_in, norm_gain)
        router_probs = jax.nn.softmax(jnp.dot(normed, w_router, preferred_element_type=jnp.float32), axis=-1)
        gate_vals = jnp.take_along_axis(router_probs, topk_idx, axis=1)
        flat_ids = topk_idx.reshape(-1)
        onehot = (flat_ids[:, None] == jnp.arange(experts)[None, :]).astype(jnp.int32)
        local_pos = jnp.sum((jnp.cumsum(onehot, axis=0) - onehot) * onehot, axis=1)
        all_counts = lax.all_gather(jnp.sum(onehot, axis=0), 'ep')
        my_rank = lax.axis_index('ep')
        lower_counts = jnp.sum(jnp.where(jnp.arange(group_size)[:, None] < my_rank, all_counts, 0), axis=0)
        global_pos = jnp.take(lower_counts, flat_ids) + local_pos
        buf_pos = jnp.where(global_pos < capacity, flat_ids * local_max + local_pos, num_slots * local_max)
        token_of = jnp.arange(tok_dev * top_k) // top_k
        row_table = jnp.full((num_slots * local_max,), tok_dev, jnp.int32).at[buf_pos].set(token_of, mode='drop')
        send_buf = jnp.take(normed, row_table, axis=0, mode='fill', fill_value=0).reshape(num_slots, local_max, hidden)
        recv_buf = lax.all_to_all(send_buf, 'ep', 0, 1, tiled=True)
        gate_proj = jnp.einsum('sch,shf->scf', recv_buf, w_gate, preferred_element_type=jnp.float32)
        up_proj = jnp.einsum('sch,shf->scf', recv_buf, w_up, preferred_element_type=jnp.float32)
        expert_act = (jax.nn.silu(gate_proj) * up_proj).astype(jnp.bfloat16)
        expert_out = jnp.einsum('scf,sfh->sch', expert_act, w_down, preferred_element_type=jnp.float32).astype(jnp.bfloat16)
        back_buf = lax.all_to_all(expert_out, 'ep', 1, 0, tiled=True)
        picked = jnp.take(back_buf.reshape(num_slots * local_max, hidden), buf_pos, axis=0, mode='fill', fill_value=0)
        picked = picked.reshape(tok_dev, top_k, hidden)
        routed = jnp.sum(gate_vals[:, :, None] * picked.astype(jnp.float32), axis=1)
        shared_val = shared_expert(normed, w_sgate, s_gate, s_up, s_down)
        return (hidden_in.astype(jnp.float32) + routed + shared_val).astype(jnp.bfloat16)

    row_spec = P(('dp', 'ep'), None)
    full_spec = P(None, None)
    slot_spec = P('ep', None, None)
    in_specs = (row_spec, row_spec, P(None), full_spec, full_spec, full_spec, full_spec, full_spec,
                slot_spec, slot_spec, slot_spec)
    return jax.shard_map(device_block, mesh=mesh, in_specs=in_specs, out_specs=row_spec, check_vma=False)
```

profile of v0, /device:TPU:21, one launch (start us, length us, event | category | flops | bytes accessed | tf_op | source)
XLA Modules:
  0.0 1598.9 jit_solution(10788474798860826234)
XLA Ops:
  0.0 0.9 copy.62
  0.9 0.2 eq.26
  1.3 18.3 %reduce-window.6 = s32[64,24,128]{2,1,0:T(8,128)S(1)} reduce-window(s32[64,24,128]{2,1,0:T(8,128)S(1)} %fusion.8, s32[]{:T(128)} %constant.50.clone.1), window={size=1x1x128 pad=0_0x0_0x127_0}, to_apply=%region_5.6 | reduce-window | flops 24969216 | bytes 1572868 | tf_op jit(solution)/shard_map/reduce-window
  19.7 0.3 slice.79
  19.9 0.4 copy.74
  20.4 0.2 reduce-window.9
  20.6 0.3 broadcast_add_fusion
  20.8 0.3 convert_reduce_fusion
  21.1 1.2 dynamic-slice
  23.0 0.2 dynamic-update-slice
  23.3 16.1 %all-reduce = s32[1024]{0:T(1024)S(1)} all-reduce(s32[1024]{0:T(1024)S(1)} %dynamic-update-slice), channel_id=2, replica_groups=mesh['dp'=4,'ep'=16] {'ep'}, use_global_device_ids=true, to_apply=%add | all-reduce | flops 1024 | bytes 8192
  39.6 0.7 fusion.20
  40.3 0.7 fusion.21
  41.0 0.2 reshape.189
  41.2 0.7 fusion.18
  41.9 0.7 fusion.19
  42.6 4.3 compare_select_fusion.3
  47.0 2.2 compare_reduce_fusion.56
  49.2 35.8 %select_select_fusion = s32[3072]{0:T(1024)S(1)} fusion(pred[3072]{0:T(1024)(128)(4,1)S(1)} %get-tuple-element.63, pred[3072]{0:T(1024)(128)(4,1)S(1)} %get-tuple-element.61, pred[3072]{0:T(1024)(128)(4,1)S(1)} %get-tuple-element.62, pred[3072]{0:T(1024)(128)(4,1)S(1)} %get-tuple-element.60, pred[3072]{0:T(1024)(128)(4,1)S(1)} %get-tuple-element.59, ...), kind=kLoop, calls=%fused_computation.113 | loop fusion | flops 175104 | bytes 199908 | tf_op jit(solution)/shard_map/jit(_take)/gather | solution.py:40
  85.0 0.5 copy-done.4
  85.6 11.8 scatter_custom_fusion
  97.4 0.7 convert_element_type.33
  98.1 2.1 fusion.1
  100.3 2.1 fusion.3
  102.4 30.9 %gather_fusion = bf16[6144,2048]{1,0:T(8,128)(2,1)} fusion(bf16[512,2048]{1,0:T(8,128)(2,1)S(1)} %fusion.3, s32[6144]{0:T(1024)S(1)} %fusion.11), kind=kCustom, calls=%fused_computation | custom fusion | bytes 50356224 | tf_op jit(solution)/shard_map/jit(_take)/gather | solution.py:44
  133.4 20.9 %broadcast_select_fusion = bf16[64,96,2048]{2,1,0:T(8,128)(2,1)} fusion(bf16[64,96,2048]{2,1,0:T(8,128)(2,1)} %bitcast.121, pred[64,96]{1,0:T(8,128)(4,1)S(1)} %broadcast_in_dim.74), kind=kLoop, calls=%fused_computation.8 | loop fusion | flops 12582912 | bytes 50337792 | tf_op jit(solution)/shard_map/jit(_take)/select_n | solution.py:44
  154.3 552.3 %all_to_all.33 = bf16[64,96,2048]{2,1,0:T(8,128)(2,1)S(1)} all-to-all(bf16[64,96,2048]{2,1,0:T(8,128)(2,1)} %broadcast_select_fusion), channel_id=1, replica_groups=mesh['dp'=4,'ep'=16] {'ep'}, dimensions={0} | all-to-all | bytes 50331648 | tf_op jit(solution)/shard_map/all_to_all | solution.py:45
  706.6 8.4 copy.71
  715.0 47.8 %fusion.23 = f32[4,1536,1408]{2,1,0:T(8,128)} fusion(bf16[4,1536,2048]{2,1,0:T(8,128)(2,1)} %bitcast.122, bf16[4,2048,1408]{2,1,0:T(8,128)(2,1)} %param.19), kind=kOutput, calls=%fused_computation.128 | convolution fusion | flops 35433480192 | bytes 82837504 | tf_op jit(solution)/shard_map/sch,shf->scf/dot_general | solution.py:46
  762.8 53.0 %fusion = bf16[4,1536,1408]{2,1,0:T(8,128)(2,1)} fusion(bf16[4,1536,2048]{2,1,0:T(8,128)(2,1)} %bitcast.123, bf16[4,2048,1408]{2,1,0:T(8,128)(2,1)} %param.20, f32[4,1536,1408]{2,1,0:T(8,128)} %fusion.23), kind=kOutput, calls=%fused_computation.7 | convolution fusion | flops 35485384704 | bytes 100139008 | tf_op jit(solution)/shard_map/sch,shf->scf/dot_general | solution.py:47
  815.8 47.9 %convolution_convert_fusion = bf16[4,1536,2048]{2,1,0:T(8,128)(2,1)} fusion(bf16[4,1536,1408]{2,1,0:T(8,128)(2,1)} %fusion, bf16[4,1408,2048]{2,1,0:T(8,128)(2,1)} %param.21), kind=kOutput, calls=%fused_computation.6 | convolution fusion | flops 35446063104 | bytes 65536000 | tf_op jit(solution)/shard_map/scf,sfh->sch/dot_general | solution.py:49
  863.7 32.1 %copy.72 = bf16[4,1536,2048]{2,0,1:T(4,128)(2,1)} copy(bf16[4,1536,2048]{2,1,0:T(8,128)(2,1)} %convolution_convert_fusion) | data formatting | bytes 50331648 | tf_op jit(solution)/shard_map/convert_element_type | solution.py:49
  895.9 6.0 all-to-all-start.1
  901.9 0.2 gather.26
  902.1 0.2 reduce_sum.63
  902.6 0.2 copy.70
  903.0 0.2 reshape.280
  903.2 0.8 fusion.22
  904.0 24.9 %gather_fusion.2 = f32[3072]{0:T(1024)S(1)} fusion(f32[512,64]{0,1:T(8,128)S(1)} %fusion.9, s32[3072]{0:T(1024)S(1)} %reshape.280), kind=kCustom, calls=%fused_computation.2 | custom fusion | bytes 49152 | tf_op jit(solution)/shard_map/jit(take_along_axis)/gather | solution.py:33
  929.0 0.2 reshape.283
  929.5 0.6 fusion.24
  930.2 11.1 fusion.25
  941.2 529.0 %all-to-all-done.1 = bf16[4,1536,2048]{2,0,1:T(4,128)(2,1)} async-done(((bf16[4,1536,2048]{2,0,1:T(4,128)(2,1)}), bf16[4,1536,2048]{2,0,1:T(4,128)(2,1)}, u32[]{:S(2)}, u32[]{:S(2)}) %all-to-all-start.1) | async-done | bytes 25165856 | tf_op jit(solution)/shard_map/all_to_all | solution.py:50
  1470.2 26.8 %copy.73 = bf16[4,16,96,2048]{3,2,0,1:T(8,128)(2,1)} copy(bf16[4,16,96,2048]{3,0,2,1:T(4,128)(2,1)} %bitcast.77) | data formatting | bytes 50331648 | tf_op jit(solution)/shard_map/all_to_all | solution.py:50
  1497.1 35.2 %gather_fusion.1 = bf16[3072,2048]{1,0:T(8,128)(2,1)} fusion(bf16[6144,2048]{1,0:T(8,128)(2,1)} %bitcast.119, s32[3072]{0:T(1024)S(1)} %broadcast_clamp_fusion), kind=kCustom, calls=%fused_computation.1 | custom fusion | bytes 25178112 | tf_op jit(solution)/shard_map/jit(_take)/gather | solution.py:51
  1532.3 20.4 %gather.31 = bf16[512,6,2048]{2,1,0:T(8,128)(2,1)} reshape(bf16[3072,2048]{1,0:T(8,128)(2,1)} %gather_fusion.1) | data formatting | bytes 25165824 | tf_op jit(solution)/shard_map/jit(_take)/gather | solution.py:51
  1552.6 21.2 %multiply_reduce_fusion = f32[512,2048]{1,0:T(8,128)} fusion(bf16[512,6,2048]{2,1,0:T(8,128)(2,1)} %gather.31, f32[512,6]{1,0:T(8,128)S(1)} %copy.61, pred[512,6]{1,0:T(8,128)(4,1)S(1)} %copy.70), kind=kLoop, calls=%fused_computation.5 | loop fusion | flops 24117248 | bytes 16792576 | tf_op jit(solution)/shard_map/reduce_sum | solution.py:53
  1573.9 24.6 %fusion.5 = bf16[512,2048]{1,0:T(8,128)(2,1)} fusion(f32[512,2048]{1,0:T(8,128)} %multiply_reduce_fusion, bf16[512,2048]{1,0:T(8,128)(2,1)} %param.11, bf16[2816,2048]{1,0:T(8,128)(2,1)} %param.18, f32[512]{0:T(512)S(1)} %add_divide_fusion, f32[512,2816]{1,0:T(8,128)} %fusion.25, bf16[512,2048]{1,0:T(8,128)(2,1)S(1)} %copy-done.2, bf16[2048,2816]{1,0:T(8,128)(2,1)} %param.17), kind=kOutput, calls=%fused_computation.17 | convolution fusion | flops 11825053696 | bytes 39323648 | tf_op jit(solution)/shard_map/dot_general | solution.py:16
  (45 shorter events, 1.4 us)
Async XLA Ops:
  0.0 903.1 %copy-start = (bf16[2048,64]{0,1:T(8,128)(2,1)S(1)}, bf16[2048,64]{0,1:T(8,128)(2,1)}, u32[]{:S(2)}) copy-start(bf16[2048,64]{0,1:T(8,128)(2,1)} %param.14) | copy-start | bytes 786436
  21.1 63.9 %copy-start.6 = (s32[3072]{0:T(1024)}, s32[3072]{0:T(1024)S(1)}, u32[]{:S(2)}) copy-start(s32[3072]{0:T(1024)S(1)} %get-tuple-element.6) | copy-start | bytes 36868
  85.0 0.6 copy-start.4
  85.6 14.6 copy-start.8
  102.4 31.0 %copy-start.1 = (bf16[512,2048]{1,0:T(8,128)(2,1)}, bf16[512,2048]{1,0:T(8,128)(2,1)S(1)}, u32[]{:S(2)}) copy-start(bf16[512,2048]{1,0:T(8,128)(2,1)S(1)} %fusion.3) | copy-start | bytes 6291460
  895.9 6.0 copy-start.5
  895.9 6.3 copy-start.7
  895.9 6.7 copy-start.3
  895.9 7.3 copy-start.2
  895.9 574.4 %all-to-all-start.1 = ((bf16[4,1536,2048]{2,0,1:T(4,128)(2,1)}), bf16[4,1536,2048]{2,0,1:T(4,128)(2,1)}, u32[]{:S(2)}, u32[]{:S(2)}) async-start(bf16[4,1536,2048]{2,0,1:T(4,128)(2,1)} %copy.72), calls=%async_computation.1 | async-start | bytes 50331648 | tf_op jit(solution)/shard_map/all_to_all | solution.py:50
  904.0 25.4 %copy-start.10 = (bf16[2048,1]{0,1:T(2,128)(2,1)S(1)}, bf16[2048,1]{0,1:T(2,128)(2,1)}, u32[]{:S(2)}) copy-start(bf16[2048,1]{0,1:T(2,128)(2,1)} %param.15) | copy-start | bytes 12292
  904.0 26.1 %copy-start.9 = (s32[3072,1]{0,1:T(1,128)S(1)}, s32[3072,1]{0,1:T(1,128)}, u32[]{:S(2)}) copy-start(s32[3072,1]{0,1:T(1,128)} %copy-done.8) | copy-start | bytes 36868
where the time goes:
time: 1610 us; the launch traced here: 1600 us
  blocking collectives  568 us (35%)
  waiting for transfers between devices  529 us (33%)
  local copies, waits for them, and re-layouts  199 us (12%)
  matrix products  186 us (12%)
  other arithmetic  109 us (7%)
    all_to_all x1, blocking collectives, device_block(): recv_buf = lax.all_to_all(send_buf, 'ep', 0, 1, tiled=True)  552 us
    all_to_all x1, waiting for transfers between devices, device_block(): back_buf = lax.all_to_all(expert_out, 'ep', 1, 0, tiled=True)  529 us
    gather x2, local copies, waits for them, and re-layouts, device_block(): jnp.take(back_buf.reshape(num_slots * local_max, hidden), buf_pos, axis=0...  55.5 us
    dot_general x1, matrix products, device_block(): jnp.einsum('sch,shf->scf', recv_buf, w_up, preferred_element_type=jnp.flo...  53 us
    dot_general x1, matrix products, device_block(): jnp.einsum('scf,sfh->sch', expert_act, w_down, preferred_element_type=jnp...  47.9 us
    dot_general x1, matrix products, device_block(): jnp.einsum('sch,shf->scf', recv_buf, w_gate, preferred_element_type=jnp.f...  47.8 us
    gather x3, other arithmetic, device_block(): global_pos = jnp.take(lower_counts, flat_ids) + local_pos  42.3 us
  transfers between devices with their start and end apart: 1, of which 1 were waited for; matrix products, arithmetic and copies ran while one was open for 2% of the time, Pallas kernels for 0%

commit v1 on v0

v1 whole, which is shorter than its diff:
```python
import functools

import jax
import jax.numpy as jnp
from jax import lax
from jax.experimental import pallas as pl
from jax.experimental.pallas import tpu as pltpu
from jax.sharding import PartitionSpec as P

CHUNKS = 2
ROW_TILE = 192
F32 = jnp.float32
BF16 = jnp.bfloat16


def rms_norm(hidden_in, norm_gain):
    x_f32 = hidden_in.astype(F32)
    inv_rms = lax.rsqrt(jnp.mean(x_f32 * x_f32, axis=-1, keepdims=True) + 1e-6)
    return (x_f32 * inv_rms * norm_gain.astype(F32)).astype(BF16)


def shared_expert(normed, w_sgate, s_gate, s_up, s_down):
    shared_act = (jax.nn.silu(jnp.dot(normed, s_gate, preferred_element_type=F32))
                  * jnp.dot(normed, s_up, preferred_element_type=F32)).astype(BF16)
    shared_val = jnp.dot(shared_act, s_down, preferred_element_type=F32)
    return jax.nn.sigmoid(jnp.dot(normed, w_sgate, preferred_element_type=F32)) * shared_val


def exclusive_count(flags):
    lead, total = flags.shape
    lanes = 128
    blocks = total // lanes
    grid = flags.astype(BF16).reshape(lead * blocks, lanes)
    upper = (jnp.arange(lanes)[:, None] < jnp.arange(lanes)[None, :]).astype(BF16)
    inner = jnp.dot(grid, upper, preferred_element_type=F32).reshape(lead, blocks, lanes)
    sums = jnp.sum(flags.reshape(lead, blocks, lanes), axis=-1)
    before = (jnp.arange(blocks)[:, None] < jnp.arange(blocks)[None, :]).astype(BF16)
    outer = jnp.dot(sums.astype(BF16), before, preferred_element_type=F32)
    return (inner + outer[:, :, None]).reshape(lead, total)


def ffn_kernel(count_ref, x_ref, gate_ref, up_ref, down_ref, out_ref):
    tiles = pl.num_programs(1)
    filled = lax.div(count_ref[pl.program_id(0)] + (ROW_TILE - 1), ROW_TILE)

    @pl.when(pl.program_id(1) >= tiles - filled)
    def _():
        rows = x_ref[0]
        gate = jnp.dot(rows, gate_ref[0], preferred_element_type=F32)
        up = jnp.dot(rows, up_ref[0], preferred_element_type=F32)
        act = (gate * jax.nn.sigmoid(gate) * up).astype(BF16)
        out_ref[0] = jnp.dot(act, down_ref[0], preferred_element_type=F32).astype(BF16)


def expert_ffn(counts, rows, w_gate, w_up, w_down):
    slots, padded, hidden = rows.shape
    ff = w_gate.shape[2]
    tiles = padded // ROW_TILE

    def row_map(e, r, count_ref):
        filled = lax.div(count_ref[e] + (ROW_TILE - 1), ROW_TILE)
        return e, jnp.maximum(r - (tiles - filled), 0), 0

    def weight_map(e, r, count_ref):
        return e, 0, 0

    return pl.pallas_call(
        ffn_kernel,
        out_shape=jax.ShapeDtypeStruct((slots, padded, hidden), BF16),
        grid_spec=pltpu.PrefetchScalarGridSpec(
            num_scalar_prefetch=1,
            grid=(slots, tiles),
            in_specs=[
                pl.BlockSpec((1, ROW_TILE, hidden), row_map),
                pl.BlockSpec((1, hidden, ff), weight_map),
                pl.BlockSpec((1, hidden, ff), weight_map),
                pl.BlockSpec((1, ff, hidden), weight_map),
            ],
            out_specs=pl.BlockSpec((1, ROW_TILE, hidden), row_map),
        ),
        compiler_params=pltpu.CompilerParams(
            dimension_semantics=("arbitrary", "arbitrary"), vmem_limit_bytes=58 * 1024 * 1024),
        cost_estimate=pl.CostEstimate(
            flops=3 * slots * padded * hidden * ff, bytes_accessed=6 * slots * hidden * ff,
            transcendentals=0),
        name="expert_ffn",
    )(counts, rows, w_gate, w_up, w_down)


def combine_kernel(slots, window, start_ref, count_ref, meta_ref, rows_ref, out_ref):
    source = pl.program_id(0)
    tokens = meta_ref.shape[0]
    padded = rows_ref.shape[1]
    lane = lax.broadcasted_iota(jnp.int32, (tokens, window), 1)
    sub = lax.broadcasted_iota(jnp.int32, (window, 1), 0)
    meta = meta_ref[...]
    for e in range(slots):
        first = lax.div(start_ref[source * slots + e], 16) * 16
        first = pl.multiple_of(jnp.minimum(first, padded - window), 16)
        rows = rows_ref[e, pl.ds(first, window), :]
        rows = jnp.where(sub + first < count_ref[e], rows, jnp.zeros_like(rows))
        wanted = meta[:, e:e + 1].astype(jnp.int32) - first
        pick = (lane == wanted).astype(F32).astype(BF16)
        term = meta[:, slots + e:slots + e + 1] * jnp.dot(pick, rows, preferred_element_type=F32)
        if e == 0:
            out_ref[0] = term
        else:
            out_ref[0] += term


def combine(starts, counts, meta, rows, window, sources):
    slots, padded, hidden = rows.shape
    tokens = meta.shape[0] // sources
    return pl.pallas_call(
        functools.partial(combine_kernel, slots, window),
        out_shape=jax.ShapeDtypeStruct((sources, tokens, hidden), F32),
        grid_spec=pltpu.PrefetchScalarGridSpec(
            num_scalar_prefetch=2,
            grid=(sources,),
            in_specs=[
                pl.BlockSpec((tokens, meta.shape[1]), lambda s, *_: (s, 0)),
                pl.BlockSpec((slots, padded, hidden), lambda s, *_: (0, 0, 0),
                             pipeline_mode=pl.Buffered(1)),
            ],
            out_specs=pl.BlockSpec((1, tokens, hidden), lambda s, *_: (s, 0, 0)),
        ),
        compiler_params=pltpu.CompilerParams(
            dimension_semantics=("arbitrary",), vmem_limit_bytes=48 * 1024 * 1024),
        cost_estimate=pl.CostEstimate(
            flops=2 * sources * tokens * slots * 256 * hidden,
            bytes_accessed=4 * sources * tokens * hidden, transcendentals=0),
        name="combine",
    )(starts, counts, meta, rows)


def solution(mesh):
    group_size = mesh.shape['ep']

    def device_block(hidden_in, topk_idx, norm_gain, w_router, w_sgate, s_gate, s_up, s_down, w_gate, w_up, w_down):
        tok_dev, hidden = hidden_in.shape
        top_k = topk_idx.shape[1]
        experts = w_router.shape[1]
        slots = w_gate.shape[0]
        capacity = (5 * tok_dev * group_size * top_k + 4 * experts - 1) // (4 * experts)
        local_max = (2 * tok_dev * top_k + experts - 1) // experts
        padded = -(-capacity // ROW_TILE) * ROW_TILE
        window = -(-local_max // 16) * 16 + 16
        part = tok_dev // CHUNKS
        my_rank = lax.axis_index('ep')

        normed = rms_norm(hidden_in, norm_gain)
        gathered = [lax.all_gather(normed[c * part:(c + 1) * part], 'ep', tiled=True) for c in range(CHUNKS)]

        logits = lax.dot_general(w_router, normed, (((0,), (1,)), ((), ())), preferred_element_type=F32)
        probs = jax.nn.softmax(logits, axis=0)
        ids = topk_idx.T
        ids_f32 = ids.astype(F32)
        gates = jnp.sum(jnp.where(ids[:, None, :] == jnp.arange(experts)[None, :, None], probs[None], 0.0), axis=1)
        route = lax.all_gather(jnp.concatenate([ids_f32, gates], axis=0), 'ep')
        all_ids, all_gates = route[:, :top_k], route[:, top_k:]

        my_slots = (my_rank * slots + jnp.arange(slots)).astype(F32)
        match = all_ids[None] == my_slots[:, None, None, None]
        hit = jnp.sum(match.astype(F32), axis=2)
        gate = jnp.sum(jnp.where(match, all_gates[None], 0.0), axis=2)
        order = exclusive_count(hit.reshape(slots, group_size * tok_dev)).reshape(hit.shape)
        kept = jnp.where(order < capacity, hit, 0.0)

        partial_sums = []
        for c in range(CHUNKS):
            kept_c = kept[:, :, c * part:(c + 1) * part].reshape(slots, group_size * part)
            gate_c = gate[:, :, c * part:(c + 1) * part].reshape(slots, group_size * part)
            place = exclusive_count(kept_c)
            place = jnp.where(kept_c > 0, place, -1.0)
            per_source = jnp.sum(kept_c.reshape(slots, group_size, part), axis=2).astype(jnp.int32)
            counts = jnp.sum(per_source, axis=1)
            starts = (jnp.cumsum(per_source, axis=1) - per_source).T.reshape(-1)
            meta = jnp.concatenate([place, gate_c], axis=0).T
            token = jnp.arange(group_size * part, dtype=jnp.int32)
            seats = jnp.arange(padded, dtype=jnp.int32).astype(F32)
            table = jnp.sum(jnp.where(place[:, None, :] == seats[None, :, None], token[None, None, :], 0), axis=2)
            rows = gathered[c].at[table.reshape(-1)].get(mode='promise_in_bounds')
            results = expert_ffn(counts, rows.reshape(slots, padded, hidden), w_gate, w_up, w_down)
            partial = combine(starts, counts, meta, results, window, group_size)
            partial_sums.append(partial.reshape(group_size * part, hidden))
        routed = [lax.psum_scatter(p, 'ep', scatter_dimension=0, tiled=True) for p in partial_sums]
        shared_in, _ = lax.optimization_barrier((normed, partial_sums[0]))
        shared_val = shared_expert(shared_in, w_sgate, s_gate, s_up, s_down)
        base = lax.optimization_barrier(hidden_in.astype(F32) + shared_val)
        return (base + jnp.concatenate(routed, axis=0)).astype(BF16)

    row_spec = P(('dp', 'ep'), None)
    full_spec = P(None, None)
    slot_spec = P('ep', None, None)
    in_specs = (row_spec, row_spec, P(None), full_spec, full_spec, full_spec, full_spec, full_spec,
                slot_spec, slot_spec, slot_spec)
    return jax.shard_map(device_block, mesh=mesh, in_specs=in_specs, out_specs=row_spec, check_vma=False)
```

time: 1610 us -> 611 us (0.38)
  blocking collectives: 568 us -> 26.4 us
  waiting for transfers between devices: 529 us -> 254 us
  Pallas kernels: 0 us -> 168 us
  matrix products: 186 us -> 37.5 us
  local copies, waits for them, and re-layouts: 199 us -> 80.3 us
  other arithmetic: 109 us -> 31.6 us
    all_to_all x1 -> x0, blocking collectives: 552 us -> none  [device_block(): recv_buf = lax.all_to_all(send_buf, 'ep', 0, 1, tiled=True)]
    all_to_all x1 -> x0, waiting for transfers between devices: 529 us -> none  [device_block(): back_buf = lax.all_to_all(expert_out, 'ep', 1, 0, tiled=True)]
    reduce_scatter x0 -> x2, waiting for transfers between devices: none -> 205 us  [device_block(): lax.psum_scatter(p, 'ep', scatter_dimension=0, tiled=True)]
    pallas_call x0 -> x4, Pallas kernels: none -> 168 us  [the longest x2 110 us: expert_ffn(): pl.pallas_call(ffn_kernel, out_shape=jax.ShapeDtypeStruct((slots, padded,...]
    dot_general x7 -> x10, matrix products: 186 us -> 37.5 us  [the longest x1 24.1 us: shared_expert(): shared_val = jnp.dot(shared_act, s_down, preferred_element_type=F32)]
    all_gather x0 -> x2, waiting for transfers between devices: none -> 48.1 us  [device_block(): lax.all_gather(normed[c * part:(c + 1) * part], 'ep', tiled=True)]
    gather x6 -> x2, other arithmetic: 42.3 us -> 0.01 us  [device_block(): rows = gathered[c].at[table.reshape(-1)].get(mode='promise_in_bounds')]
    gather x14 -> x2, local copies, waits for them, and re-layouts: 115 us -> 74.8 us  [device_block(): rows = gathered[c].at[table.reshape(-1)].get(mode='promise_in_bounds')]
  transfers between devices with their start and end apart: 1 -> 4, of which waited for: 1 -> 3; matrix products, arithmetic and copies ran while one was open for 2% -> 22% of each run, Pallas kernels for 0% -> 27%
where the time goes in v1:
time: 611 us; the launch traced here: 612 us
  waiting for transfers between devices  254 us (42%)
  Pallas kernels  168 us (27%)
  local copies, waits for them, and re-layouts  80.3 us (13%)
  matrix products  37.5 us (6%)
  other arithmetic  31.6 us (5%)
  blocking collectives  26.4 us (4%)
  between operations  13.5 us (2%)
    reduce_scatter x2, waiting for transfers between devices, device_block(): lax.psum_scatter(p, 'ep', scatter_dimension=0, tiled=True)  205 us
    pallas_call x2, Pallas kernels, expert_ffn(): pl.pallas_call(ffn_kernel, out_shape=jax.ShapeDtypeStruct((slots, padded,...  110 us
    gather x2, local copies, waits for them, and re-layouts, device_block(): rows = gathered[c].at[table.reshape(-1)].get(mode='promise_in_bounds')  74.8 us
    pallas_call x2, Pallas kernels, combine(): pl.pallas_call(functools.partial(combine_kernel, slots, window), out_shap...  57.9 us
    all_gather x2, waiting for transfers between devices, device_block(): lax.all_gather(normed[c * part:(c + 1) * part], 'ep', tiled=True)  48.1 us
    all_gather x1, blocking collectives, device_block(): route = lax.all_gather(jnp.concatenate([ids_f32, gates], axis=0), 'ep')  26.4 us
    dot_general x1, matrix products, shared_expert(): shared_val = jnp.dot(shared_act, s_down, preferred_element_type=F32)  24.1 us
    reduce_sum x1, other arithmetic, device_block(): jnp.sum(jnp.where(place[:, None, :] == seats[None, :, None], token[None,...  18.2 us
  transfers between devices with their start and end apart: 4, of which 3 were waited for; matrix products, arithmetic and copies ran while one was open for 22% of the time, Pallas kernels for 27%

profile of v1, /device:TPU:21, one launch (start us, length us, event | category | flops | bytes accessed | tf_op | source)
XLA Modules:
  0.0 611.7 jit_solution(2109500091675728595)
XLA Ops:
  6.6 0.7 convert_element_type.80
  7.3 2.1 fusion
  9.4 2.1 fusion.2
  11.5 1.6 fusion.25
  13.3 0.7 all-gather.5.cloned.1.call-update
  14.1 0.8 fusion.27
  15.0 0.1 select_reduce_fusion.2
  15.1 26.4 %all-gather.1 = f32[16,12,512]{2,1,0:T(8,128)S(1)} all-gather(f32[1,12,512]{2,1,0:T(8,128)S(1)} %maximum_bitcast_fusion), channel_id=2, replica_groups=mesh['dp'=4,'ep'=16] {'ep'}, dimensions={0}, use_global_device_ids=true | all-gather | bytes 417792 | tf_op jit(solution)/shard_map/all_gather | solution.py:159
  41.5 0.1 copy.56
  41.7 0.1 copy.61
  41.8 0.2 fusion.8
  42.0 0.1 reduce_sum.130
  42.2 0.1 copy.67
  42.3 0.2 fusion.17
  42.4 0.2 fusion.4
  42.7 0.1 slice_reduce_fusion
  42.8 0.1 reduce_sum.133
  43.0 0.1 reduce_sum.138
  43.1 0.1 fusion.19
  43.3 0.1 fusion.6
  43.4 0.2 fusion.18
  43.5 0.1 fusion.5
  43.6 0.2 bitcast_select_fusion
  43.8 18.2 %select_reduce_fusion = (s32[4,960]{1,0:T(4,128)S(1)}, s32[4,960]{1,0:T(4,128)S(1)}) fusion(f32[4,4096]{1,0:T(4,128)S(1)} %get-tuple-element.29, f32[960]{0:T(1024)S(1)} %iota_convert_fusion, f32[4,4096]{1,0:T(4,128)S(1)} %get-tuple-element.30), kind=kLoop, calls=%fused_computation.2 | loop fusion | flops 94364160 | bytes 165632 | tf_op jit(solution)/shard_map/reduce_sum | solution.py:181
  62.1 0.1 reshape.191
  62.3 0.6 copy.66
  62.9 0.2 reduce_window_sum.18
  63.1 0.7 convert_reduce_fusion
  63.9 0.1 reshape.187.start_ref
  64.0 48.1 %all-gather.7.cloned.1.call-done = bf16[4096,2048]{1,0:T(8,128)(2,1)} async-done(((bf16[256,2048]{1,0:T(8,128)(2,1)}), bf16[4096,2048]{1,0:T(8,128)(2,1)}) %all-gather.7.cloned.1.call-update) | async-done | bytes 16777232 | tf_op jit(solution)/shard_map/all_gather | solution.py:152
  112.1 37.4 %gather_fusion.1 = bf16[3840,2048]{1,0:T(8,128)(2,1)} fusion(bf16[4096,2048]{1,0:T(8,128)(2,1)} %all-gather.7.cloned.1.call-done, s32[4096]{0:T(1024)S(1)} %pad_clamp_fusion), kind=kCustom, calls=%fused_computation.1 | custom fusion | bytes 31472640 | tf_op jit(solution)/shard_map/gather | solution.py:182
  149.5 55.2 %expert_ffn.3.rows_ref = bf16[4,960,2048]{2,1,0:T(8,128)(2,1)} custom-call(s32[4]{0:T(128)} %get-tuple-element.23.count_ref, bf16[4,960,2048]{2,1,0:T(8,128)(2,1)} %bitcast.58, bf16[4,2048,1408]{2,1,0:T(8,128)(2,1)} %gate_ref.3, bf16[4,2048,1408]{2,1,0:T(8,128)(2,1)} %up_ref.3, bf16[4,1408,2048]{2,1,0:T(8,128)(2,1)} %down_ref.3), custom_call_target="tpu_custom_call" | custom-call | flops 33218887680 | bytes 69206016 | tf_op jit(solution)/shard_map/expert_ffn/pallas_call | solution.py:67
  204.7 29.0 %combine.3 = f32[16,256,2048]{2,1,0:T(8,128)} custom-call(s32[64]{0:T(128)S(1)} %reshape.187.start_ref, s32[4]{0:T(128)S(1)} %copy-done.2, f32[4096,8]{1,0:T(8,128)S(1)} %bitcast.54, bf16[4,960,2048]{2,1,0:T(8,128)(2,1)} %expert_ffn.3.rows_ref), custom_call_target="tpu_custom_call" | custom-call | flops 17179869184 | bytes 33554432 | tf_op jit(solution)/shard_map/combine/pallas_call | solution.py:114
  233.7 0.3 reduce-scatter.3.cloned.1.call-start
  234.0 0.1 reshape.183
  234.1 0.2 reduce_window_sum.17
  234.4 0.6 copy.62
  235.0 0.7 convert_reduce_fusion.1
  236.0 37.4 %gather_fusion = bf16[3840,2048]{1,0:T(8,128)(2,1)} fusion(bf16[4096,2048]{1,0:T(8,128)(2,1)} %all-gather.5.cloned.1.call-done, s32[4096]{0:T(1024)S(1)} %pad_clamp_fusion.1), kind=kCustom, calls=%fused_computation | custom fusion | bytes 31472640 | tf_op jit(solution)/shard_map/gather | solution.py:182
  273.4 55.2 %expert_ffn.2.rows_ref = bf16[4,960,2048]{2,1,0:T(8,128)(2,1)} custom-call(s32[4]{0:T(128)} %get-tuple-element.25.count_ref, bf16[4,960,2048]{2,1,0:T(8,128)(2,1)} %bitcast.59, bf16[4,2048,1408]{2,1,0:T(8,128)(2,1)} %gate_ref.3, bf16[4,2048,1408]{2,1,0:T(8,128)(2,1)} %up_ref.3, bf16[4,1408,2048]{2,1,0:T(8,128)(2,1)} %down_ref.3), custom_call_target="tpu_custom_call" | custom-call | flops 33218887680 | bytes 69206016 | tf_op jit(solution)/shard_map/expert_ffn/pallas_call | solution.py:67
  328.6 28.9 %combine.2 = f32[16,256,2048]{2,1,0:T(8,128)} custom-call(s32[64]{0:T(128)S(1)} %reshape.179.start_ref, s32[4]{0:T(128)S(1)} %copy-done.3, f32[4096,8]{1,0:T(8,128)S(1)} %bitcast.55, bf16[4,960,2048]{2,1,0:T(8,128)(2,1)} %expert_ffn.2.rows_ref), custom_call_target="tpu_custom_call" | custom-call | flops 17179869184 | bytes 33554432 | tf_op jit(solution)/shard_map/combine/pallas_call | solution.py:114
  357.6 1.5 copy-done.5
  359.1 0.6 fusion.28
  359.7 11.2 %fusion.29 = f32[512,2816]{1,0:T(8,128)} fusion(bf16[512,2048]{1,0:T(8,128)(2,1)S(1)} %copy-done.5, bf16[2048,2816]{1,0:T(8,128)(2,1)} %param.16), kind=kOutput, calls=%fused_computation.72 | convolution fusion | flops 5905580032 | bytes 19398656 | tf_op jit(solution)/shard_map/dot_general | solution.py:23
  371.0 24.1 %convert_add_fusion = f32[512,2048]{1,0:T(8,128)} fusion(bf16[512,2048]{1,0:T(8,128)(2,1)} %param.11, bf16[2816,2048]{1,0:T(8,128)(2,1)} %param.18, f32[512]{0:T(512)S(1)} %add_divide_fusion, f32[512,2816]{1,0:T(8,128)} %fusion.29, bf16[512,2048]{1,0:T(8,128)(2,1)S(1)} %copy-done.5, bf16[2048,2816]{1,0:T(8,128)(2,1)} %param.17), kind=kOutput, calls=%fused_computation.4 | convolution fusion | flops 11822956544 | bytes 37226496 | tf_op jit(solution)/shard_map/dot_general | solution.py:25
  395.0 21.9 %reduce-scatter.5.cloned.1.call-done = f32[256,2048]{1,0:T(8,128)} async-done(((f32[4096,2048]{1,0:T(8,128)}), f32[256,2048]{1,0:T(8,128)}) %reduce-scatter.5.cloned.1.call-update) | async-done | bytes 2097168 | tf_op jit(solution)/shard_map/reduce_scatter | solution.py:186
  416.9 182.8 %reduce-scatter.3.cloned.1.call-done = f32[256,2048]{1,0:T(8,128)} async-done(((f32[4096,2048]{1,0:T(8,128)}), f32[256,2048]{1,0:T(8,128)}) %reduce-scatter.3.cloned.1.call-update) | async-done | bytes 2097168 | tf_op jit(solution)/shard_map/reduce_scatter | solution.py:186
  599.8 5.4 fusion.3
  (53 shorter events, 1.2 us)
Async XLA Ops:
  6.5 7.5 %copy-start = (bf16[2048,64]{0,1:T(8,128)(2,1)S(1)}, bf16[2048,64]{0,1:T(8,128)(2,1)}, u32[]{:S(2)}) copy-start(bf16[2048,64]{0,1:T(8,128)(2,1)} %param.14) | copy-start | bytes 786436
  6.6 105.6 %all-gather.7.cloned.1.call-start = ((), (), s32[]{:S(2)}) async-start(), calls=%async_computation.4 | async-start | bytes 17825792 | tf_op jit(solution)/shard_map/all_gather | solution.py:152
  9.4 5.6 copy-start.6
  11.5 30.1 %copy-start.4 = (bf16[512,2048]{1,0:T(8,128)(2,1)}, bf16[512,2048]{1,0:T(8,128)(2,1)S(1)}, u32[]{:S(2)}) copy-start(bf16[512,2048]{1,0:T(8,128)(2,1)S(1)} %fusion.2) | copy-start | bytes 6291460
  13.2 222.8 %all-gather.5.cloned.1.call-start = ((), (), s32[]{:S(2)}) async-start(), calls=%async_computation.2 | async-start | bytes 17825792 | tf_op jit(solution)/shard_map/all_gather | solution.py:152
  14.0 402.9 %reduce-scatter.5.cloned.1.call-start = ((), (), s32[]{:S(2)}) async-start(), calls=%async_computation.5 | async-start | bytes 35651584 | tf_op jit(solution)/shard_map/reduce_scatter | solution.py:186
  149.5 55.2 %copy-start.2 = (s32[4]{0:T(128)S(1)}, s32[4]{0:T(128)}, u32[]{:S(2)}) copy-start(s32[4]{0:T(128)} %get-tuple-element.23.count_ref) | copy-start | bytes 52
  233.7 366.0 %reduce-scatter.3.cloned.1.call-start = ((), (), s32[]{:S(2)}) async-start(), calls=%async_computation.3 | async-start | bytes 35651584 | tf_op jit(solution)/shard_map/reduce_scatter | solution.py:186
  273.4 55.2 %copy-start.3 = (s32[4]{0:T(128)S(1)}, s32[4]{0:T(128)}, u32[]{:S(2)}) copy-start(s32[4]{0:T(128)} %get-tuple-element.25.count_ref) | copy-start | bytes 52
  357.5 1.6 copy-start.5
  357.5 1.6 copy-start.7
  371.0 234.2 %copy-start.1 = (bf16[2048,64]{0,1:T(8,128)(2,1)S(1)}, bf16[2048,64]{0,1:T(8,128)(2,1)}, u32[]{:S(2)}) copy-start(bf16[2048,64]{0,1:T(8,128)(2,1)} %param.14) | copy-start | bytes 786436
Sparse Core Ops, SparseCore 0:
  13.3 98.7 all-gather.6
  113.8 90.4 all-gather.4
  233.8 183.0 reduce-scatter.4
  419.2 180.5 reduce-scatter.2

commit v2 on v1

--- a/solution.py
+++ b/solution.py
@@ -7,7 +7,7 @@
 from jax.experimental.pallas import tpu as pltpu
 from jax.sharding import PartitionSpec as P
 
-CHUNKS = 2
+SPLIT = (3, 5)
 ROW_TILE = 192
 F32 = jnp.float32
 BF16 = jnp.bfloat16
@@ -16,7 +16,7 @@
 def rms_norm(hidden_in, norm_gain):
     x_f32 = hidden_in.astype(F32)
     inv_rms = lax.rsqrt(jnp.mean(x_f32 * x_f32, axis=-1, keepdims=True) + 1e-6)
-    return (x_f32 * inv_rms * norm_gain.astype(F32)).astype(BF16)
+    return (x_f32 * inv_rms * norm_gain.astype(F32)).astype(BF16), inv_rms
 
 
 def shared_expert(normed, w_sgate, s_gate, s_up, s_down):
@@ -37,6 +37,51 @@
     before = (jnp.arange(blocks)[:, None] < jnp.arange(blocks)[None, :]).astype(BF16)
     outer = jnp.dot(sums.astype(BF16), before, preferred_element_type=F32)
     return (inner + outer[:, :, None]).reshape(lead, total)
+
+
+def pack_kernel(slots, window, start_ref, seat_ref, gain_ref, x_ref, out_ref):
+    source = pl.program_id(0)
+    tokens = x_ref.shape[0]
+    padded = out_ref.shape[1]
+    sub = lax.broadcasted_iota(jnp.int32, (window, tokens), 0)
+    row = lax.broadcasted_iota(jnp.int32, (window, 1), 0)
+    inv_rms = seat_ref[0, slots:slots + 1, :]
+    gain = gain_ref[...]
+    for e in range(slots):
+        start = start_ref[source * slots + e]
+        first = pl.multiple_of(jnp.minimum(lax.div(start, 16) * 16, padded - window), 16)
+        chosen = sub == seat_ref[0, e:e + 1, :].astype(jnp.int32) - first
+        pick = chosen.astype(F32).astype(BF16)
+        scale = jnp.sum(jnp.where(chosen, inv_rms, 0.0), axis=1, keepdims=True)
+        rows = jnp.dot(pick, x_ref[...], preferred_element_type=F32)
+        rows = (rows * scale * gain).astype(BF16)
+        old = out_ref[e, pl.ds(first, window), :]
+        out_ref[e, pl.ds(first, window), :] = jnp.where(row + first >= start, rows, old)
+
+
+def pack_rows(starts, seats, gain, x_rows, slots, padded, window, sources):
+    hidden = x_rows.shape[1]
+    tokens = x_rows.shape[0] // sources
+    return pl.pallas_call(
+        functools.partial(pack_kernel, slots, window),
+        out_shape=jax.ShapeDtypeStruct((slots, padded, hidden), BF16),
+        grid_spec=pltpu.PrefetchScalarGridSpec(
+            num_scalar_prefetch=1,
+            grid=(sources,),
+            in_specs=[
+                pl.BlockSpec((1,) + seats.shape[1:], lambda s, *_: (s, 0, 0)),
+                pl.BlockSpec((1, hidden), lambda s, *_: (0, 0)),
+                pl.BlockSpec((tokens, hidden), lambda s, *_: (s, 0)),
+            ],
+            out_specs=pl.BlockSpec((slots, padded, hidden), lambda s, *_: (0, 0, 0)),
+        ),
+        compiler_params=pltpu.CompilerParams(
+            dimension_semantics=("arbitrary",), vmem_limit_bytes=52 * 1024 * 1024),
+        cost_estimate=pl.CostEstimate(
+            flops=2 * sources * tokens * slots * 256 * hidden,
+            bytes_accessed=2 * sources * tokens * hidden, transcendentals=0),
+        name="pack_rows",
+    )(starts, seats, gain, x_rows)
 
 
 def ffn_kernel(count_ref, x_ref, gate_ref, up_ref, down_ref, out_ref):
@@ -145,19 +190,20 @@
         local_max = (2 * tok_dev * top_k + experts - 1) // experts
         padded = -(-capacity // ROW_TILE) * ROW_TILE
         window = -(-local_max // 16) * 16 + 16
-        part = tok_dev // CHUNKS
+        bounds = [tok_dev * sum(SPLIT[:c]) // sum(SPLIT) for c in range(len(SPLIT) + 1)]
         my_rank = lax.axis_index('ep')
 
-        normed = rms_norm(hidden_in, norm_gain)
-        gathered = [lax.all_gather(normed[c * part:(c + 1) * part], 'ep', tiled=True) for c in range(CHUNKS)]
+        normed, inv_rms = rms_norm(hidden_in, norm_gain)
+        gain = norm_gain.astype(F32)[None]
+        gathered = [lax.all_gather(hidden_in[lo:hi], 'ep', tiled=True) for lo, hi in zip(bounds, bounds[1:])]
 
         logits = lax.dot_general(w_router, normed, (((0,), (1,)), ((), ())), preferred_element_type=F32)
         probs = jax.nn.softmax(logits, axis=0)
         ids = topk_idx.T
         ids_f32 = ids.astype(F32)
         gates = jnp.sum(jnp.where(ids[:, None, :] == jnp.arange(experts)[None, :, None], probs[None], 0.0), axis=1)
-        route = lax.all_gather(jnp.concatenate([ids_f32, gates], axis=0), 'ep')
-        all_ids, all_gates = route[:, :top_k], route[:, top_k:]
+        route = lax.all_gather(jnp.concatenate([ids_f32, gates, inv_rms.T], axis=0), 'ep')
+        all_ids, all_gates, all_inv = route[:, :top_k], route[:, top_k:2 * top_k], route[:, 2 * top_k:]
 
         my_slots = (my_rank * slots + jnp.arange(slots)).astype(F32)
         match = all_ids[None] == my_slots[:, None, None, None]
@@ -167,20 +213,20 @@
         kept = jnp.where(order < capacity, hit, 0.0)
 
         partial_sums = []
-        for c in range(CHUNKS):
-            kept_c = kept[:, :, c * part:(c + 1) * part].reshape(slots, group_size * part)
-            gate_c = gate[:, :, c * part:(c + 1) * part].reshape(slots, group_size * part)
+        for c, (lo, hi) in enumerate(zip(bounds, bounds[1:])):
+            part = hi - lo
+            kept_c = kept[:, :, lo:hi].reshape(slots, group_size * part)
+            gate_c = gate[:, :, lo:hi].reshape(slots, group_size * part)
             place = exclusive_count(kept_c)
             place = jnp.where(kept_c > 0, place, -1.0)
             per_source = jnp.sum(kept_c.reshape(slots, group_size, part), axis=2).astype(jnp.int32)
             counts = jnp.sum(per_source, axis=1)
             starts = (jnp.cumsum(per_source, axis=1) - per_source).T.reshape(-1)
             meta = jnp.concatenate([place, gate_c], axis=0).T
-            token = jnp.arange(group_size * part, dtype=jnp.int32)
-            seats = jnp.arange(padded, dtype=jnp.int32).astype(F32)
-            table = jnp.sum(jnp.where(place[:, None, :] == seats[None, :, None], token[None, None, :], 0), axis=2)
-            rows = gathered[c].at[table.reshape(-1)].get(mode='promise_in_bounds')
-            results = expert_ffn(counts, rows.reshape(slots, padded, hidden), w_gate, w_up, w_down)
+            seats = jnp.concatenate(
+                [place.reshape(slots, group_size, part).transpose(1, 0, 2), all_inv[:, :, lo:hi]], axis=1)
+            rows = pack_rows(starts, seats, gain, gathered[c], slots, padded, window, group_size)
+            results = expert_ffn(counts, rows, w_gate, w_up, w_down)
             partial = combine(starts, counts, meta, results, window, group_size)
             partial_sums.append(partial.reshape(group_size * part, hidden))
         routed = [lax.psum_scatter(p, 'ep', scatter_dimension=0, tiled=True) for p in partial_sums]

time: 611 us -> 578 us (0.946)
  local copies, waits for them, and re-layouts: 80.3 us -> 10.9 us
  Pallas kernels: 168 us -> 213 us
  other arithmetic: 31.6 us -> 9.6 us
  waiting for transfers between devices: 254 us -> 264 us
    gather x2 -> x0, local copies, waits for them, and re-layouts: 74.8 us -> none  [device_block(): rows = gathered[c].at[table.reshape(-1)].get(mode='promise_in_bounds')]
    pallas_call x0 -> x2, Pallas kernels: none -> 52.5 us  [pack_rows(): pl.pallas_call(functools.partial(pack_kernel, slots, window), out_shape=j...]
    reduce_sum x2 -> x0, other arithmetic: 18.3 us -> none  [the longest x1 18.2 us: device_block(): jnp.sum(jnp.where(place[:, None, :] == seats[None, :, None], token[None,...]
    all_gather x2, waiting for transfers between devices: 48.1 us -> 59.7 us  [device_block(): lax.all_gather(hidden_in[lo:hi], 'ep', tiled=True)]
    pallas_call x2, Pallas kernels: 110 us -> 102 us  [expert_ffn(): pl.pallas_call(ffn_kernel, out_shape=jax.ShapeDtypeStruct((slots, padded,...]
  transfers between devices with their start and end apart: 4 -> 4, of which waited for: 3 -> 3; matrix products, arithmetic and copies ran while one was open for 22% -> 8% of each run, Pallas kernels for 27% -> 37%
where the time goes in v2:
time: 578 us; the launch traced here: 577 us
  waiting for transfers between devices  264 us (46%)
  Pallas kernels  213 us (37%)
  matrix products  39 us (7%)
  blocking collectives  27 us (5%)
  between operations  13.5 us (2%)
  local copies, waits for them, and re-layouts  10.9 us (2%)
  other arithmetic  9.6 us (2%)
    reduce_scatter x2, waiting for transfers between devices, device_block(): lax.psum_scatter(p, 'ep', scatter_dimension=0, tiled=True)  204 us
    pallas_call x2, Pallas kernels, expert_ffn(): pl.pallas_call(ffn_kernel, out_shape=jax.ShapeDtypeStruct((slots, padded,...  102 us
    all_gather x2, waiting for transfers between devices, device_block(): lax.all_gather(hidden_in[lo:hi], 'ep', tiled=True)  59.7 us
    pallas_call x2, Pallas kernels, combine(): pl.pallas_call(functools.partial(combine_kernel, slots, window), out_shap...  58.3 us
    pallas_call x2, Pallas kernels, pack_rows(): pl.pallas_call(functools.partial(pack_kernel, slots, window), out_shape=j...  52.5 us
    all_gather x1, blocking collectives, device_block(): lax.all_gather(jnp.concatenate([ids_f32, gates, inv_rms.T], axis=0), 'ep')  27 us
    dot_general x1, matrix products, shared_expert(): shared_val = jnp.dot(shared_act, s_down, preferred_element_type=F32)  24 us
    dot_general x1, matrix products, shared_expert(): jnp.dot(normed, s_gate, preferred_element_type=F32)  12.7 us
  transfers between devices with their start and end apart: 4, of which 3 were waited for; matrix products, arithmetic and copies ran while one was open for 8% of the time, Pallas kernels for 37%

profile of v2, /device:TPU:21, one launch (start us, length us, event | category | flops | bytes accessed | tf_op | source)
XLA Modules:
  0.0 577.3 jit_solution(12182878791264282372)
XLA Ops:
  6.6 2.3 slice.38
  9.0 2.5 slice.42
  11.7 0.5 fusion
  12.2 0.6 fusion.2
  12.7 1.3 copy-done.6
  14.1 0.8 fusion.24
  14.9 0.1 select_reduce_fusion
  15.1 27.0 %all-gather.1 = f32[16,13,512]{2,1,0:T(8,128)S(1)} all-gather(f32[1,13,512]{2,1,0:T(8,128)S(1)} %maximum_bitcast_fusion), channel_id=2, replica_groups=mesh['dp'=4,'ep'=16] {'ep'}, dimensions={0}, use_global_device_ids=true | all-gather | bytes 452608 | tf_op jit(solution)/shard_map/all_gather | solution.py:205
  42.1 0.1 copy.57
  42.2 0.1 copy.64
  42.4 0.2 fusion.6
  42.6 0.1 reduce_sum.112
  42.7 0.1 fusion.16
  42.8 0.2 fusion.4
  43.1 0.1 copy_select_fusion
  43.4 0.1 fusion.19
  43.6 0.1 convolution_add_fusion.2
  43.7 0.1 reshape.117
  43.8 0.1 fusion.9
  44.0 0.2 reduce_window_sum.17
  44.2 0.7 convert_reduce_fusion.1
  45.1 0.1 gt.22
  45.4 0.5 copy.65
  45.9 43.1 %all-gather.5.cloned.1.call-done.x_ref = bf16[3072,2048]{1,0:T(8,128)(2,1)} async-done(((bf16[192,2048]{1,0:T(8,128)(2,1)}), bf16[3072,2048]{1,0:T(8,128)(2,1)}) %all-gather.5.cloned.1.call-update) | async-done | bytes 12582928 | tf_op jit(solution)/shard_map/all_gather | solution.py:198
  89.1 23.6 %pack_rows.2.x_ref = bf16[4,960,2048]{2,1,0:T(8,128)(2,1)} custom-call(s32[64]{0:T(128)S(1)} %reshape.113.start_ref, f32[16,5,192]{2,1,0:T(8,128)S(1)} %pad_maximum_fusion.2.seat_ref, f32[1,2048]{1,0:T(1,128)S(1)} %bitcast.46, bf16[3072,2048]{1,0:T(8,128)(2,1)} %all-gather.5.cloned.1.call-done.x_ref), custom_call_target="tpu_custom_call" | custom-call | flops 12884901888 | bytes 12582912 | tf_op jit(solution)/shard_map/pack_rows/pallas_call | solution.py:65
  112.7 43.1 %expert_ffn.2.rows_ref = bf16[4,960,2048]{2,1,0:T(8,128)(2,1)} custom-call(s32[4]{0:T(128)} %get-tuple-element.19.count_ref, bf16[4,960,2048]{2,1,0:T(8,128)(2,1)} %pack_rows.2.x_ref, bf16[4,2048,1408]{2,1,0:T(8,128)(2,1)} %gate_ref.3, bf16[4,2048,1408]{2,1,0:T(8,128)(2,1)} %up_ref.3, bf16[4,1408,2048]{2,1,0:T(8,128)(2,1)} %down_ref.3), custom_call_target="tpu_custom_call" | custom-call | flops 33218887680 | bytes 69206016 | tf_op jit(solution)/shard_map/expert_ffn/pallas_call | solution.py:112
  155.8 25.0 %combine.2 = f32[16,192,2048]{2,1,0:T(8,128)} custom-call(s32[64]{0:T(128)S(1)} %reshape.113.start_ref, s32[4]{0:T(128)S(1)} %copy-done.2, f32[3072,8]{1,0:T(8,128)S(1)} %bitcast.45, bf16[4,960,2048]{2,1,0:T(8,128)(2,1)} %expert_ffn.2.rows_ref), custom_call_target="tpu_custom_call" | custom-call | flops 12884901888 | bytes 25165824 | tf_op jit(solution)/shard_map/combine/pallas_call | solution.py:159
  180.9 0.2 reduce-scatter.5.cloned.1.call-start
  181.1 0.1 slice.48
  181.2 0.1 slice.50
  181.7 0.1 fusion.18
  181.8 0.2 convolution_add_fusion.1
  182.1 0.2 fusion.8
  182.4 0.2 reduce_window_sum.18
  182.5 0.7 convert_reduce_fusion
  183.4 0.1 gt.25
  183.5 0.1 reshape.123
  183.7 0.7 copy.71
  184.5 16.5 %all-gather.7.cloned.1.call-done.x_ref = bf16[5120,2048]{1,0:T(8,128)(2,1)} async-done(((bf16[320,2048]{1,0:T(8,128)(2,1)}), bf16[5120,2048]{1,0:T(8,128)(2,1)}) %all-gather.7.cloned.1.call-update) | async-done | bytes 20971536 | tf_op jit(solution)/shard_map/all_gather | solution.py:198
  201.0 28.9 %pack_rows.3.x_ref = bf16[4,960,2048]{2,1,0:T(8,128)(2,1)} custom-call(s32[64]{0:T(128)S(1)} %reshape.120.start_ref, f32[16,5,320]{2,1,0:T(8,128)S(1)} %pad_maximum_fusion.seat_ref, f32[1,2048]{1,0:T(1,128)S(1)} %bitcast.47, bf16[5120,2048]{1,0:T(8,128)(2,1)} %all-gather.7.cloned.1.call-done.x_ref), custom_call_target="tpu_custom_call" | custom-call | flops 21474836480 | bytes 20971520 | tf_op jit(solution)/shard_map/pack_rows/pallas_call | solution.py:65
  229.9 59.1 %expert_ffn.3.rows_ref = bf16[4,960,2048]{2,1,0:T(8,128)(2,1)} custom-call(s32[4]{0:T(128)} %get-tuple-element.17.count_ref, bf16[4,960,2048]{2,1,0:T(8,128)(2,1)} %pack_rows.3.x_ref, bf16[4,2048,1408]{2,1,0:T(8,128)(2,1)} %gate_ref.3, bf16[4,2048,1408]{2,1,0:T(8,128)(2,1)} %up_ref.3, bf16[4,1408,2048]{2,1,0:T(8,128)(2,1)} %down_ref.3), custom_call_target="tpu_custom_call" | custom-call | flops 33218887680 | bytes 69206016 | tf_op jit(solution)/shard_map/expert_ffn/pallas_call | solution.py:112
  289.0 33.3 %combine.3 = f32[16,320,2048]{2,1,0:T(8,128)} custom-call(s32[64]{0:T(128)S(1)} %reshape.120.start_ref, s32[4]{0:T(128)S(1)} %copy-done.3, f32[5120,8]{1,0:T(8,128)S(1)} %bitcast.44, bf16[4,960,2048]{2,1,0:T(8,128)(2,1)} %expert_ffn.3.rows_ref), custom_call_target="tpu_custom_call" | custom-call | flops 21474836480 | bytes 41943040 | tf_op jit(solution)/shard_map/combine/pallas_call | solution.py:159
  322.4 1.5 copy-done.7
  323.9 0.6 fusion.25
  324.6 12.7 %fusion.26 = f32[512,2816]{1,0:T(8,128)} fusion(bf16[512,2048]{1,0:T(8,128)(2,1)} %copy-done.6, bf16[2048,2816]{1,0:T(8,128)(2,1)} %param.16), kind=kOutput, calls=%fused_computation.63 | convolution fusion | flops 5905580032 | bytes 19398656 | tf_op jit(solution)/shard_map/dot_general | solution.py:23
  337.3 24.0 %convert_add_fusion = f32[512,2048]{1,0:T(8,128)} fusion(bf16[512,2048]{1,0:T(8,128)(2,1)S(1)} %copy-done.5, bf16[2816,2048]{1,0:T(8,128)(2,1)} %param.18, f32[512]{0:T(512)S(1)} %add_divide_fusion, f32[512,2816]{1,0:T(8,128)} %fusion.26, bf16[512,2048]{1,0:T(8,128)(2,1)} %copy-done.6, bf16[2048,2816]{1,0:T(8,128)(2,1)} %param.17), kind=kOutput, calls=%fused_computation | convolution fusion | flops 11822956544 | bytes 37226496 | tf_op jit(solution)/shard_map/dot_general | solution.py:25
  361.4 204.0 %reduce-scatter.5.cloned.1.call-done = f32[320,2048]{1,0:T(8,128)} async-done(((f32[5120,2048]{1,0:T(8,128)}), f32[320,2048]{1,0:T(8,128)}) %reduce-scatter.5.cloned.1.call-update) | async-done | bytes 2621456 | tf_op jit(solution)/shard_map/reduce_scatter | solution.py:232
  565.4 5.4 fusion.3
  (67 shorter events, 2.1 us)
Async XLA Ops:
  6.5 7.5 %copy-start = (bf16[2048,64]{0,1:T(8,128)(2,1)S(1)}, bf16[2048,64]{0,1:T(8,128)(2,1)}, u32[]{:S(2)}) copy-start(bf16[2048,64]{0,1:T(8,128)(2,1)} %param.14) | copy-start | bytes 786436
  6.6 5.1 copy-start.4
  6.6 5.1 copy-start.10
  6.6 82.5 %all-gather.5.cloned.1.call-start = ((), (), s32[]{:S(2)}) async-start(), calls=%async_computation.2 | async-start | bytes 13369344 | tf_op jit(solution)/shard_map/all_gather | solution.py:198
  8.9 192.2 %all-gather.7.cloned.1.call-start = ((), (), s32[]{:S(2)}) async-start(), calls=%async_computation.4 | async-start | bytes 22282240 | tf_op jit(solution)/shard_map/all_gather | solution.py:198
  11.5 349.8 %reduce-scatter.3.cloned.1.call-start = ((), (), s32[]{:S(2)}) async-start(), calls=%async_computation.3 | async-start | bytes 26738688 | tf_op jit(solution)/shard_map/reduce_scatter | solution.py:232
  11.7 3.3 copy-start.8
  12.7 1.3 copy-start.6
  112.7 43.1 %copy-start.2 = (s32[4]{0:T(128)S(1)}, s32[4]{0:T(128)}, u32[]{:S(2)}) copy-start(s32[4]{0:T(128)} %get-tuple-element.19.count_ref) | copy-start | bytes 52
  180.9 384.5 %reduce-scatter.5.cloned.1.call-start = ((), (), s32[]{:S(2)}) async-start(), calls=%async_computation.5 | async-start | bytes 44564480 | tf_op jit(solution)/shard_map/reduce_scatter | solution.py:232
  229.9 59.1 %copy-start.3 = (s32[4]{0:T(128)S(1)}, s32[4]{0:T(128)}, u32[]{:S(2)}) copy-start(s32[4]{0:T(128)} %get-tuple-element.17.count_ref) | copy-start | bytes 52
  322.3 1.6 copy-start.7
  322.3 1.6 copy-start.9
  324.6 12.7 %copy-start.5 = (bf16[512,2048]{1,0:T(8,128)(2,1)S(1)}, bf16[512,2048]{1,0:T(8,128)(2,1)}, u32[]{:S(2)}) copy-start(bf16[512,2048]{1,0:T(8,128)(2,1)} %param.11) | copy-start | bytes 6291460
  337.3 233.4 %copy-start.1 = (bf16[2048,64]{0,1:T(8,128)(2,1)S(1)}, bf16[2048,64]{0,1:T(8,128)(2,1)}, u32[]{:S(2)}) copy-start(bf16[2048,64]{0,1:T(8,128)(2,1)} %param.14) | copy-start | bytes 786436
Sparse Core Ops, SparseCore 0:
  9.0 80.0 all-gather.4
  90.7 110.2 all-gather.6
  203.4 137.2 reduce-scatter.2
  342.9 222.4 reduce-scatter.4
